TPU v7x, 32 devices: a whole 2x2x4 slice. The times are simulated.
32 devices in a mesh: mode: 8 (over y, x, core), tm: 4 (over z).
Axes of the slice: x: 2, y: 2, z: 4, core: 2. Of those that a mesh axis runs over, the one named last changes fastest.
Arguments:
- field: float32 [2, 128, 65536], P(None, 'mode', 'tm'), may hold values from -1.8 to 1.8
- beta: float32 [3, 128], P(None, 'mode'), may hold values from -1 to 1
- quartets: int32 [4, 1024], replicated, may hold values from 0 to 127
- intersections: float32 [1024], replicated, may hold values from -0.12 to 0.12
Outputs:
- field_out: float32 [2, 128, 65536], P(None, 'mode', 'tm')
- errors: float32 [2, 128], P(None, 'mode')
All inputs are finite; a program needn't handle non-finite values.
Results may differ from a plain program's by a relative error of at most 0.0003.
Values sent between devices are 32-bit elements; how exact they have to be, the bound alone decides.
A program may use at most 128 MiB of HBM per device.

v0:
```python
import math
import jax
import jax.numpy as jnp
from jax import lax
from jax.sharding import PartitionSpec as P

RADIX = 256
STEPS = 2
epsilon = 1e-06


def phase_of(offset, slope, curve, frequency):
    return math.pi * offset + 300.0 * slope * frequency + 3000.0 * curve * frequency * frequency


def triple_product(left_field, middle_field, conj_field):
    prod_re = left_field[0] * middle_field[0] - left_field[1] * middle_field[1]
    prod_im = left_field[0] * middle_field[1] + left_field[1] * middle_field[0]
    out_re = prod_re * conj_field[0] + prod_im * conj_field[1]
    out_im = prod_im * conj_field[0] - prod_re * conj_field[1]
    return (out_re, out_im)


def contract(form, first_operand, second_operand):
    return jnp.einsum(form, first_operand, second_operand, precision=lax.Precision.HIGHEST)


def rotate(real_part, imag_part, angle):
    cosine = jnp.cos(angle)
    sine_part = jnp.sin(angle)
    return (real_part * cosine - imag_part * sine_part, real_part * sine_part + imag_part * cosine)


def dft_tables(length):
    positions = lax.iota(jnp.int32, length)
    product = positions[:, None] * positions[None, :] % length
    angle = -2.0 * math.pi / length * product.astype(jnp.float32)
    return (jnp.cos(angle), jnp.sin(angle))


def to_columns(state):
    return lax.all_to_all(state, "tm", split_axis=3, concat_axis=2, tiled=True)


def to_rows(state):
    return lax.all_to_all(state, "tm", split_axis=2, concat_axis=3, tiled=True)


def linear_step(state, beta, table_re, table_im):
    radix_size = table_re.shape[0]
    total_time = radix_size * radix_size
    cols_local = state.shape[3]
    tm_index = lax.axis_index("tm")
    head_re = contract("ka,mab->mkb", table_re, state[0]) - contract(
        "ka,mab->mkb", table_im, state[1]
    )
    head_im = contract("ka,mab->mkb", table_re, state[1]) + contract(
        "ka,mab->mkb", table_im, state[0]
    )
    column = tm_index * cols_local + lax.iota(jnp.int32, cols_local)
    row_position = lax.iota(jnp.int32, radix_size)
    twist = (
        -2.0
        * math.pi
        / total_time
        * (row_position[:, None] * column[None, :] % total_time).astype(jnp.float32)
    )
    head_re, head_im = rotate(head_re, head_im, twist[None])
    turned = lax.all_to_all(
        jnp.stack([head_re, head_im]), "tm", split_axis=2, concat_axis=3, tiled=True
    )
    spec_re = contract("mcb,kb->mck", turned[0], table_re) - contract(
        "mcb,kb->mck", turned[1], table_im
    )
    spec_im = contract("mcb,kb->mck", turned[1], table_re) + contract(
        "mcb,kb->mck", turned[0], table_im
    )
    rows_local = turned.shape[2]
    first_index = tm_index * rows_local + lax.iota(jnp.int32, rows_local)
    wave = first_index[:, None] + radix_size * row_position[None, :]
    signed = jnp.where(wave < total_time // 2, wave, wave - total_time)
    frequency = signed.astype(jnp.float32) / (total_time / 2)
    angle = phase_of(
        beta[0][:, None, None], beta[1][:, None, None], beta[2][:, None, None], frequency[None]
    )
    spec_re, spec_im = rotate(spec_re, spec_im, angle)
    back_re = contract("mck,kb->mcb", spec_re, table_re) + contract(
        "mck,kb->mcb", spec_im, table_im
    )
    back_im = contract("mck,kb->mcb", spec_im, table_re) - contract(
        "mck,kb->mcb", spec_re, table_im
    )
    untwist = (
        2.0
        * math.pi
        / total_time
        * (first_index[:, None] * row_position[None, :] % total_time).astype(jnp.float32)
    )
    back_re, back_im = rotate(back_re, back_im, untwist[None])
    gathered = lax.all_to_all(
        jnp.stack([back_re, back_im]), "tm", split_axis=3, concat_axis=2, tiled=True
    )
    scale = 1.0 / total_time
    out_re = (
        contract("ka,mkb->mab", table_re, gathered[0])
        + contract("ka,mkb->mab", table_im, gathered[1])
    ) * scale
    out_im = (
        contract("ka,mkb->mab", table_re, gathered[1])
        - contract("ka,mkb->mab", table_im, gathered[0])
    ) * scale
    return jnp.stack([out_re, out_im])


def kerr_term(fields, quartets, intersections):
    count = quartets.shape[1]
    block_size = min(512, count)
    blocks = count // block_size
    grouped = quartets.reshape(4, blocks, block_size).transpose(1, 0, 2)
    weights = intersections.reshape(blocks, block_size)
    modes_all = fields.shape[1]
    mode_ids = lax.iota(jnp.int32, modes_all)

    def accumulate(running, block_item):
        indices, weight = block_item
        out_re, out_im = triple_product(
            jnp.take(fields, indices[1], axis=1),
            jnp.take(fields, indices[2], axis=1),
            jnp.take(fields, indices[3], axis=1),
        )
        owner = (indices[0][None, :] == mode_ids[:, None]).astype(jnp.float32) * weight[None, :]
        add_re = contract("pq,qt->pt", owner, -out_im)
        add_im = contract("pq,qt->pt", owner, out_re)
        return (running + jnp.stack([add_re, add_im]), None)

    running, unused = lax.scan(accumulate, jnp.zeros_like(fields), (grouped, weights))
    return running


def kerr_step(flat, quartets, intersections):
    spread = lax.all_to_all(flat, "mode", split_axis=2, concat_axis=1, tiled=True)
    first = kerr_term(spread, quartets, intersections)
    second = kerr_term(spread + first, quartets, intersections)
    updated = spread + 0.5 * (first + second)
    estimate = 0.5 * (second - first)
    returned, estimate_home = (
        lax.all_to_all(updated, "mode", split_axis=1, concat_axis=2, tiled=True),
        lax.all_to_all(estimate, "mode", split_axis=1, concat_axis=2, tiled=True),
    )
    error_part = jnp.sum(estimate_home * estimate_home, axis=(0, 2))
    field_part = jnp.sum(returned * returned, axis=(0, 2))
    return (returned, error_part, field_part)


def shards(field, beta, quartets, intersections):
    modes_local = field.shape[1]
    time_local = field.shape[2]
    table_re, table_im = dft_tables(RADIX)
    state = field.reshape(2, modes_local, time_local // RADIX, RADIX)
    state = to_columns(state)
    error_rows = []
    for step_index in range(STEPS):
        columns = state
        columns = linear_step(columns, beta, table_re, table_im)
        updated, error_part, field_part = kerr_step(
            columns.reshape(2, modes_local, time_local), quartets, intersections
        )
        error_sq, field_sq = lax.psum((error_part, field_part), "tm")
        error_rows.append(jnp.sqrt(error_sq / (field_sq + epsilon)))
        state = updated.reshape(columns.shape)
    state = to_rows(state)
    errors = jnp.stack(error_rows)
    return (state.reshape(2, modes_local, time_local), errors)


def solution(mesh):
    placed = (P(None, "mode", "tm"), P(None, "mode"), P(), P())
    return jax.shard_map(
        shards,
        mesh=mesh,
        in_specs=placed,
        out_specs=(P(None, "mode", "tm"), P(None, "mode")),
        check_vma=False,
    )
```

profile of v0, /device:TPU:18, one launch (start us, length us, event | category | flops | bytes accessed | tf_op | source)
XLA Modules:
  0.0 1882.4 jit_solution(8491664908036585077)
XLA Ops:
  18.4 44.6 %all-to-all-done = f32[4,1,131072]{2,1,0:T(1,128)S(1)} async-done(((f32[4,1,131072]{2,1,0:T(1,128)}), f32[4,1,131072]{2,1,0:T(1,128)S(1)}, u32[]{:S(2)}, u32[]{:S(2)}) %all-to-all-start) | async-done | bytes 2097184 | tf_op jit(solution)/shard_map/all_to_all | solution.py:42
  133.5 44.1 %all-to-all-done.1 = f32[4,1,131072]{2,1,0:T(1,128)} async-done(((f32[4,1,131072]{2,1,0:T(1,128)}), f32[4,1,131072]{2,1,0:T(1,128)}, u32[]{:S(2)}, u32[]{:S(2)}) %all-to-all-start.1) | async-done | bytes 2097184 | tf_op jit(solution)/shard_map/all_to_all | solution.py:69
  231.1 51.6 %all_to_all.174 = f32[4,1,131072]{2,1,0:T(1,128)} all-to-all(f32[4,1,131072]{2,1,0:T(1,128)S(1)} %reshape.495), channel_id=1, replica_groups=mesh['mode'=8,'tm'=4] {'tm'}, dimensions={0} | all-to-all | bytes 4194304 | tf_op jit(solution)/shard_map/all_to_all | solution.py:100
  337.0 24.7 %reshape.497 = f32[8,1,65536]{2,1,0:T(1,128)} reshape(f32[16384,2,16]{2,1,0:T(2,128)} %bitcast.446) | data formatting | bytes 4194304
  366.8 25.0 %all-to-all-done.3 = f32[8,1,65536]{2,1,0:T(1,128)} async-done(((f32[8,1,65536]{2,1,0:T(1,128)}), f32[8,1,65536]{2,1,0:T(1,128)}, u32[]{:S(2)}, u32[]{:S(2)}) %all-to-all-start.3) | async-done | bytes 2097184 | tf_op jit(solution)/shard_map/all_to_all | solution.py:141
  399.1 28.6 %reshape.498 = f32[16384,2,16]{2,1,0:T(2,128)} reshape(f32[8,65536]{1,0:T(8,128)S(1)} %reduce.13) | data formatting | bytes 4194304
  427.7 21.6 %copy.201 = f32[2,16,8,2048]{3,1,2,0:T(8,128)} copy(f32[2,16,8,2048]{1,0,3,2:T(2,128)} %bitcast.447) | data formatting | bytes 4194304 | tf_op jit(solution)/shard_map/all_to_all | solution.py:141
  452.5 210.8 %while.44 = (s32[]{:T(128)}, f32[2,128,2048]{2,1,0:T(8,128)}, s32[2,4,512]{2,1,0:T(4,128)S(1)}, f32[2,512]{1,0:T(2,128)S(1)}, f32[2,128,2048]{2,0,1:T(2,128)S(1)}, /*index=5*/s32[]{:T(128)}, s32[]{:T(128)}, s32[]{}, s32[]{}, s32[]{}) while((s32[]{:T(128)}, f32[2,128,2048]{2,1,0:T(8,128)}, s32[2,4,512]{2,1,0:T(4,128)S(1)}, ...), condition=%wide.region_1.3_spmd.clone, body=%wide.region_0.2_spmd.clone.sunk | while | flops 3243000320 | bytes 234956048 | solution.py:136
  484.7 19.5 %gather_fusion.1 = f32[512,2,2048]{2,1,0:T(2,128)} fusion(f32[2,128,2048]{2,0,1:T(2,128)S(1)} %get-tuple-element.665, s32[1024]{0:T(1024)S(1)} %pad_clamp_fusion.25), kind=kCustom, calls=%fused_computation.clone.clone.1 | custom fusion | bytes 16779264 | tf_op jit(solution)/shard_map/while/body/eval_jaxpr/jit(_take)/gather | solution.py:127
  517.7 19.7 %gather_fusion.2 = f32[512,2,2048]{2,1,0:T(2,128)} fusion(f32[2,128,2048]{2,0,1:T(2,128)S(1)} %get-tuple-element.665, s32[1024]{0:T(1024)S(1)} %pad_clamp_fusion.26), kind=kCustom, calls=%fused_computation.2.clone.clone.1 | custom fusion | bytes 16779264 | tf_op jit(solution)/shard_map/while/body/eval_jaxpr/jit(_take)/gather | solution.py:129
  588.5 19.8 %gather_fusion.1 = f32[512,2,2048]{2,1,0:T(2,128)} fusion(f32[2,128,2048]{2,0,1:T(2,128)S(1)} %get-tuple-element.665, s32[1024]{0:T(1024)S(1)} %pad_clamp_fusion.25), kind=kCustom, calls=%fused_computation.clone.clone.1 | custom fusion | bytes 16779264 | tf_op jit(solution)/shard_map/while/body/eval_jaxpr/jit(_take)/gather | solution.py:127
  667.4 215.6 %while.45 = (s32[]{:T(128)}, f32[2,128,2048]{2,1,0:T(8,128)}, s32[2,4,512]{2,1,0:T(4,128)S(1)}, f32[2,512]{1,0:T(2,128)S(1)}, f32[2,128,2048]{2,0,1:T(2,128)S(1)}, /*index=5*/s32[]{:T(128)}, s32[]{:T(128)}, s32[]{}, s32[]{}, s32[]{}) while((s32[]{:T(128)}, f32[2,128,2048]{2,1,0:T(8,128)}, s32[2,4,512]{2,1,0:T(4,128)S(1)}, ...), condition=%wide.region_3.5_spmd.clone, body=%wide.region_2.4_spmd.clone.sunk | while | flops 3243000320 | bytes 234956048 | solution.py:136
  702.6 19.8 %gather_fusion.4 = f32[512,2,2048]{2,1,0:T(2,128)} fusion(f32[2,128,2048]{2,0,1:T(2,128)S(1)} %get-tuple-element.695, s32[1024]{0:T(1024)S(1)} %pad_clamp_fusion.28), kind=kCustom, calls=%fused_computation.3.clone.clone.1 | custom fusion | bytes 16779264 | tf_op jit(solution)/shard_map/while/body/eval_jaxpr/jit(_take)/gather | solution.py:127
  806.5 19.5 %gather_fusion.4 = f32[512,2,2048]{2,1,0:T(2,128)} fusion(f32[2,128,2048]{2,0,1:T(2,128)S(1)} %get-tuple-element.695, s32[1024]{0:T(1024)S(1)} %pad_clamp_fusion.28), kind=kCustom, calls=%fused_computation.3.clone.clone.1 | custom fusion | bytes 16779264 | tf_op jit(solution)/shard_map/while/body/eval_jaxpr/jit(_take)/gather | solution.py:127
  839.5 19.7 %gather_fusion.5 = f32[512,2,2048]{2,1,0:T(2,128)} fusion(f32[2,128,2048]{2,0,1:T(2,128)S(1)} %get-tuple-element.695, s32[1024]{0:T(1024)S(1)} %pad_clamp_fusion.29), kind=kCustom, calls=%fused_computation.5.clone.clone.1 | custom fusion | bytes 16779264 | tf_op jit(solution)/shard_map/while/body/eval_jaxpr/jit(_take)/gather | solution.py:129
  889.7 29.1 %all_to_all.175 = f32[2,128,2048]{2,0,1:T(2,128)S(1)} all-to-all(f32[2,128,2048]{2,0,1:T(2,128)S(1)} %copy.171), channel_id=1, replica_groups=mesh['mode'=8,'tm'=4] {'mode'}, dimensions={1} | all-to-all | bytes 4194304 | tf_op jit(solution)/shard_map/all_to_all | solution.py:147
  956.1 51.8 %all_to_all.176 = f32[4,1,131072]{2,1,0:T(1,128)} all-to-all(f32[4,1,131072]{2,1,0:T(1,128)S(1)} %reshape.499), channel_id=1, replica_groups=mesh['mode'=8,'tm'=4] {'tm'}, dimensions={0} | all-to-all | bytes 4194304 | tf_op jit(solution)/shard_map/all_to_all | solution.py:69
  1061.5 51.0 %all_to_all.177 = f32[4,1,131072]{2,1,0:T(1,128)} all-to-all(f32[4,1,131072]{2,1,0:T(1,128)S(1)} %reshape.501), channel_id=1, replica_groups=mesh['mode'=8,'tm'=4] {'tm'}, dimensions={0} | all-to-all | bytes 4194304 | tf_op jit(solution)/shard_map/all_to_all | solution.py:100
  1166.4 24.8 %reshape.503 = f32[8,1,65536]{2,1,0:T(1,128)} reshape(f32[16384,2,16]{2,1,0:T(2,128)} %bitcast.448) | data formatting | bytes 4194304
  1198.9 22.2 %all-to-all-done.7 = f32[8,1,65536]{2,1,0:T(1,128)} async-done(((f32[8,1,65536]{2,1,0:T(1,128)}), f32[8,1,65536]{2,1,0:T(1,128)}, u32[]{:S(2)}, u32[]{:S(2)}) %all-to-all-start.7) | async-done | bytes 2097184 | tf_op jit(solution)/shard_map/all_to_all | solution.py:141
  1234.4 28.7 %reshape.504 = f32[16384,2,16]{2,1,0:T(2,128)} reshape(f32[8,65536]{1,0:T(8,128)S(1)} %reduce.16) | data formatting | bytes 4194304
  1263.1 21.6 %copy.203 = f32[2,16,8,2048]{3,1,2,0:T(8,128)} copy(f32[2,16,8,2048]{1,0,3,2:T(2,128)} %bitcast.449) | data formatting | bytes 4194304 | tf_op jit(solution)/shard_map/all_to_all | solution.py:141
  1288.0 210.6 %while.46 = (s32[]{:T(128)}, f32[2,128,2048]{2,1,0:T(8,128)}, s32[2,4,512]{2,1,0:T(4,128)S(1)}, f32[2,512]{1,0:T(2,128)S(1)}, f32[2,128,2048]{2,0,1:T(2,128)S(1)}, /*index=5*/s32[]{:T(128)}, s32[]{:T(128)}, s32[]{}, s32[]{}, s32[]{}) while((s32[]{:T(128)}, f32[2,128,2048]{2,1,0:T(8,128)}, s32[2,4,512]{2,1,0:T(4,128)S(1)}, ...), condition=%wide.region_5.7_spmd.clone, body=%wide.region_4.6_spmd.clone.sunk | while | flops 3243000320 | bytes 234956048 | solution.py:136
  1320.0 19.8 %gather_fusion.7 = f32[512,2,2048]{2,1,0:T(2,128)} fusion(f32[2,128,2048]{2,0,1:T(2,128)S(1)} %get-tuple-element.725, s32[1024]{0:T(1024)S(1)} %pad_clamp_fusion.31), kind=kCustom, calls=%fused_computation.6.clone.clone.1 | custom fusion | bytes 16779264 | tf_op jit(solution)/shard_map/while/body/eval_jaxpr/jit(_take)/gather | solution.py:127
  1424.0 19.5 %gather_fusion.7 = f32[512,2,2048]{2,1,0:T(2,128)} fusion(f32[2,128,2048]{2,0,1:T(2,128)S(1)} %get-tuple-element.725, s32[1024]{0:T(1024)S(1)} %pad_clamp_fusion.31), kind=kCustom, calls=%fused_computation.6.clone.clone.1 | custom fusion | bytes 16779264 | tf_op jit(solution)/shard_map/while/body/eval_jaxpr/jit(_take)/gather | solution.py:127
  1456.9 19.7 %gather_fusion.8 = f32[512,2,2048]{2,1,0:T(2,128)} fusion(f32[2,128,2048]{2,0,1:T(2,128)S(1)} %get-tuple-element.725, s32[1024]{0:T(1024)S(1)} %pad_clamp_fusion.32), kind=kCustom, calls=%fused_computation.8.clone.clone.1 | custom fusion | bytes 16779264 | tf_op jit(solution)/shard_map/while/body/eval_jaxpr/jit(_take)/gather | solution.py:129
  1502.7 229.3 %while.47 = (s32[]{:T(128)}, f32[2,128,2048]{2,1,0:T(8,128)}, s32[2,4,512]{2,1,0:T(4,128)S(1)}, f32[2,512]{1,0:T(2,128)S(1)}, f32[2,128,2048]{2,0,1:T(2,128)S(1)}, /*index=5*/s32[]{:T(128)}, s32[]{:T(128)}, s32[]{}, s32[]{}, s32[]{}) while((s32[]{:T(128)}, f32[2,128,2048]{2,1,0:T(8,128)}, s32[2,4,512]{2,1,0:T(4,128)S(1)}, ...), condition=%wide.region_7.9_spmd.clone, body=%wide.region_6.8_spmd.clone.sunk | while | flops 3243000320 | bytes 234956048 | solution.py:136
  1538.0 30.0 %gather_fusion.10 = f32[512,2,2048]{2,1,0:T(2,128)} fusion(f32[2,128,2048]{2,0,1:T(2,128)S(1)} %get-tuple-element.755, s32[1024]{0:T(1024)S(1)} %pad_clamp_fusion.34), kind=kCustom, calls=%fused_computation.9.clone.clone.1 | custom fusion | bytes 16779264 | tf_op jit(solution)/shard_map/while/body/eval_jaxpr/jit(_take)/gather | solution.py:127
  1581.4 19.7 %gather_fusion.11 = f32[512,2,2048]{2,1,0:T(2,128)} fusion(f32[2,128,2048]{2,0,1:T(2,128)S(1)} %get-tuple-element.755, s32[1024]{0:T(1024)S(1)} %pad_clamp_fusion.35), kind=kCustom, calls=%fused_computation.11.clone.clone.1 | custom fusion | bytes 16779264 | tf_op jit(solution)/shard_map/while/body/eval_jaxpr/jit(_take)/gather | solution.py:129
  1652.1 19.7 %gather_fusion.10 = f32[512,2,2048]{2,1,0:T(2,128)} fusion(f32[2,128,2048]{2,0,1:T(2,128)S(1)} %get-tuple-element.755, s32[1024]{0:T(1024)S(1)} %pad_clamp_fusion.34), kind=kCustom, calls=%fused_computation.9.clone.clone.1 | custom fusion | bytes 16779264 | tf_op jit(solution)/shard_map/while/body/eval_jaxpr/jit(_take)/gather | solution.py:127
  1748.7 20.6 %all-to-all-done.8 = f32[2,128,2048]{2,0,1:T(2,128)S(1)} async-done(((f32[2,128,2048]{2,0,1:T(2,128)}), f32[2,128,2048]{2,0,1:T(2,128)S(1)}, u32[]{:S(2)}, u32[]{:S(2)}) %all-to-all-start.8) | async-done | bytes 2097184 | tf_op jit(solution)/shard_map/all_to_all | solution.py:147
  1817.5 39.8 %all-reduce = (f32[16]{0:T(128)S(1)}, f32[16]{0:T(128)S(1)}, f32[16]{0:T(128)S(1)}, f32[16]{0:T(128)S(1)}) all-reduce(f32[16]{0:T(128)S(1)} %reduce_sum.56, f32[16]{0:T(128)S(1)} %multiply_reduce_fusion, f32[16]{0:T(128)S(1)} %reduce_sum.52, f32[16]{0:T(128)S(1)} %multiply_reduce_fusion.2), channel_id=1, replica_groups=mesh['mode'=8,'tm'=4] {'tm'}, use_global_device_ids=true, to_apply=%region_15.17 | all-reduce | flops 64 | bytes 512 | tf_op jit(solution)/shard_map/psum | solution.py:168
  (396 shorter events, 1078.4 us)
Async XLA Ops:
  12.9 50.1 %all-to-all-start = ((f32[4,1,131072]{2,1,0:T(1,128)}), f32[4,1,131072]{2,1,0:T(1,128)S(1)}, u32[]{:S(2)}, u32[]{:S(2)}) async-start(f32[4,1,131072]{2,1,0:T(1,128)} %reshape.491), calls=%async_computation | async-start | bytes 4194304 | tf_op jit(solution)/shard_map/all_to_all | solution.py:42
  18.4 86.7 %copy-start.27 = (f32[256,64]{0,1:T(8,128)}, f32[256,64]{0,1:T(8,128)S(1)}, u32[]{:S(2)}) copy-start(f32[256,64]{0,1:T(8,128)S(1)} %get-tuple-element.433) | copy-start | bytes 196612
  18.4 86.7 %copy-start.29 = (f32[256,64]{0,1:T(8,128)}, f32[256,64]{0,1:T(8,128)S(1)}, u32[]{:S(2)}) copy-start(f32[256,64]{0,1:T(8,128)S(1)} %get-tuple-element.434) | copy-start | bytes 196612
  119.9 13.2 copy-start.40
  125.4 52.2 %all-to-all-start.1 = ((f32[4,1,131072]{2,1,0:T(1,128)}), f32[4,1,131072]{2,1,0:T(1,128)}, u32[]{:S(2)}, u32[]{:S(2)}) async-start(f32[4,1,131072]{2,1,0:T(1,128)} %reshape.493), calls=%async_computation.1 | async-start | bytes 4194304 | tf_op jit(solution)/shard_map/all_to_all | solution.py:69
  133.1 74.7 %copy-start.33 = (f32[16]{0:T(128)}, f32[16]{0:T(128)S(1)}, u32[]{:S(2)}) copy-start(f32[16]{0:T(128)S(1)} %get-tuple-element.427) | copy-start | bytes 196
  133.1 74.7 %copy-start.35 = (f32[16]{0:T(128)}, f32[16]{0:T(128)S(1)}, u32[]{:S(2)}) copy-start(f32[16]{0:T(128)S(1)} %get-tuple-element.428) | copy-start | bytes 196
  133.1 74.7 %copy-start.37 = (f32[16]{0:T(128)}, f32[16]{0:T(128)S(1)}, u32[]{:S(2)}) copy-start(f32[16]{0:T(128)S(1)} %get-tuple-element.429) | copy-start | bytes 196
  133.5 74.3 %copy-start.25 = (f32[64,256]{1,0:T(8,128)}, f32[64,256]{1,0:T(8,128)S(1)}, u32[]{:S(2)}) copy-start(f32[64,256]{1,0:T(8,128)S(1)} %get-tuple-element.432) | copy-start | bytes 196612
  133.5 86.2 %copy-start.21 = (f32[64,256]{1,0:T(8,128)}, f32[64,256]{1,0:T(8,128)S(1)}, u32[]{:S(2)}) copy-start(f32[64,256]{1,0:T(8,128)S(1)} %get-tuple-element.430) | copy-start | bytes 196612
  133.5 86.2 %copy-start.23 = (f32[64,256]{1,0:T(8,128)}, f32[64,256]{1,0:T(8,128)S(1)}, u32[]{:S(2)}) copy-start(f32[64,256]{1,0:T(8,128)S(1)} %get-tuple-element.431) | copy-start | bytes 196612
  361.7 30.1 %all-to-all-start.3 = ((f32[8,1,65536]{2,1,0:T(1,128)}), f32[8,1,65536]{2,1,0:T(1,128)}, u32[]{:S(2)}, u32[]{:S(2)}) async-start(f32[8,1,65536]{2,1,0:T(1,128)} %reshape.497), calls=%async_computation.3 | async-start | bytes 4194304 | tf_op jit(solution)/shard_map/all_to_all | solution.py:141
  537.4 9.2 copy-start
  537.5 9.2 copy-start.1
  641.2 9.2 copy-start
  641.2 9.2 copy-start.1
  755.3 9.2 copy-start.2
  755.4 9.2 copy-start.3
  859.2 9.2 copy-start.2
  859.2 9.2 copy-start.3
  930.9 11.7 copy-start.28
  930.9 11.7 copy-start.30
  1191.2 29.9 %all-to-all-start.7 = ((f32[8,1,65536]{2,1,0:T(1,128)}), f32[8,1,65536]{2,1,0:T(1,128)}, u32[]{:S(2)}, u32[]{:S(2)}) async-start(f32[8,1,65536]{2,1,0:T(1,128)} %reshape.503), calls=%async_computation.7 | async-start | bytes 4194304 | tf_op jit(solution)/shard_map/all_to_all | solution.py:141
  1221.1 518.9 %all-to-all-start.10 = ((f32[2,128,2048]{2,0,1:T(2,128)}), f32[2,128,2048]{2,0,1:T(2,128)}, u32[]{:S(2)}, u32[]{:S(2)}) async-start(f32[2,128,2048]{2,0,1:T(2,128)} %copy.193), calls=%async_computation.10 | async-start | bytes 4194304 | tf_op jit(solution)/shard_map/all_to_all | solution.py:148
  1476.6 9.2 copy-start.4
  1476.6 9.2 copy-start.5
  1704.7 9.2 copy-start.6
  1704.7 9.2 copy-start.7
  1739.9 29.3 %all-to-all-start.8 = ((f32[2,128,2048]{2,0,1:T(2,128)}), f32[2,128,2048]{2,0,1:T(2,128)S(1)}, u32[]{:S(2)}, u32[]{:S(2)}) async-start(f32[2,128,2048]{2,0,1:T(2,128)} %copy.188), calls=%async_computation.8 | async-start | bytes 4194304 | tf_op jit(solution)/shard_map/all_to_all | solution.py:147
  1769.3 31.0 %all-to-all-start.11 = ((f32[2,128,2048]{2,0,1:T(2,128)}), f32[2,128,2048]{2,0,1:T(2,128)}, u32[]{:S(2)}, u32[]{:S(2)}) async-start(f32[2,128,2048]{2,0,1:T(2,128)} %copy.194), calls=%async_computation.11 | async-start | bytes 4194304 | tf_op jit(solution)/shard_map/all_to_all | solution.py:148
  1794.5 16.0 copy-start.14
  1800.2 57.6 %all-to-all-start.9 = ((f32[4,1,131072]{2,1,0:T(1,128)}), f32[4,1,131072]{2,1,0:T(1,128)}, u32[]{:S(2)}, u32[]{:S(2)}) async-start(f32[4,1,131072]{2,1,0:T(1,128)} %reshape.505), calls=%async_computation.9 | async-start | bytes 4194304 | tf_op jit(solution)/shard_map/all_to_all | solution.py:46
  (29 other events, 197.8 us)
where the time goes:
time: 1890 us; the launch traced here: 1880 us
  local copies, waits for them, and re-layouts  878 us (46%)
  other arithmetic  397 us (21%)
  blocking collectives  223 us (12%)
  waiting for transfers between devices  162 us (9%)
  matrix products  148 us (8%)
  starting transfers between devices  46.1 us (2%)
  loops' own time  25.8 us (1%)
    unnamed x79, local copies, waits for them, and re-layouts  174 us
    gather x8, local copies, waits for them, and re-layouts, accumulate(): jnp.take(fields, indices[1], axis=1)  168 us
    gather x8, local copies, waits for them, and re-layouts, accumulate(): jnp.take(fields, indices[3], axis=1)  157 us
    gather x8, local copies, waits for them, and re-layouts, accumulate(): jnp.take(fields, indices[2], axis=1)  155 us
    dot_general x44, matrix products, contract(): jnp.einsum(form, first_operand, second_operand, precision=lax.Precision.H...  138 us
    all_to_all x2, blocking collectives, linear_step(): lax.all_to_all(jnp.stack([back_re, back_im]), 'tm', split_axis=3, concat_...  103 us
    select_n x8, other arithmetic, accumulate(): jnp.take(fields, indices[2], axis=1)  99.3 us
    select_n x16, other arithmetic, accumulate(): jnp.take(fields, indices[3], axis=1)  73.6 us
  transfers between devices with their start and end apart: 8, of which 6 were waited for; matrix products, arithmetic and copies ran while one was open for 28% of the time, Pallas kernels for 0%

commit v1 on v0

--- a/solution.py
+++ b/solution.py
@@ -138,7 +138,16 @@
 
 
 def kerr_step(flat, quartets, intersections):
-    spread = lax.all_to_all(flat, "mode", split_axis=2, concat_axis=1, tiled=True)
+    g_now, reply = (lax.axis_size("mode"), lax.axis_index("mode"))
+    view_out = flat.shape[2] // g_now
+    extra = jnp.roll(flat, -reply * view_out, axis=2)
+    rack = [lax.slice_in_dim(extra, 0, view_out, axis=2)]
+    for m in range(1, g_now):
+        last = lax.slice_in_dim(extra, m * view_out, (m + 1) * view_out, axis=2)
+        rack.append(
+            lax.ppermute(last, axis_name="mode", perm=[(w, (w + m) % g_now) for w in range(g_now)])
+        )
+    spread = jnp.roll(jnp.concatenate(rack[::-1], axis=1), (reply + 1) * rack[0].shape[1], axis=1)
     first = kerr_term(spread, quartets, intersections)
     second = kerr_term(spread + first, quartets, intersections)
     updated = spread + 0.5 * (first + second)

time: 1890 us -> 1730 us (0.915)
  local copies, waits for them, and re-layouts: 878 us -> 701 us
  blocking collectives: 223 us -> 174 us
  waiting for transfers between devices: 162 us -> 211 us
  starting transfers between devices: 46.1 us -> 73.7 us
    unnamed x79 -> x95, local copies, waits for them, and re-layouts: 174 us -> 71.8 us
    all_to_all x2 -> x1, blocking collectives: 103 us -> 51 us  [linear_step(): lax.all_to_all(jnp.stack([back_re, back_im]), 'tm', split_axis=3, concat_...]
    ppermute x0 -> x14, waiting for transfers between devices: none -> 51.5 us  [kerr_step(): lax.ppermute(last, axis_name='mode', perm=[(w, (w + m) % g_now) for w in...]
    all_to_all x2 -> x0, local copies, waits for them, and re-layouts: 43.2 us -> none  [kerr_step(): lax.all_to_all(flat, 'mode', split_axis=2, concat_axis=1, tiled=True)]
    another operation x6 -> x4, local copies, waits for them, and re-layouts: 34.2 us -> 6.61 us  [linear_step(): return jnp.stack([out_re, out_im])]
    all_to_all x2 -> x1, waiting for transfers between devices: 47.2 us -> 44.3 us  [linear_step(): lax.all_to_all(jnp.stack([back_re, back_im]), 'tm', split_axis=3, concat_...]
  transfers between devices with their start and end apart: 8 -> 21, of which waited for: 6 -> 13; matrix products, arithmetic and copies ran while one was open for 28% -> 27% of each run, Pallas kernels for 0% -> 0%
where the time goes in v1:
time: 1730 us; the launch traced here: 1720 us
  local copies, waits for them, and re-layouts  701 us (41%)
  other arithmetic  384 us (22%)
  waiting for transfers between devices  211 us (12%)
  blocking collectives  174 us (10%)
  matrix products  151 us (9%)
  starting transfers between devices  73.7 us (4%)
  loops' own time  26.1 us (2%)
    gather x8, local copies, waits for them, and re-layouts, accumulate(): jnp.take(fields, indices[1], axis=1)  167 us
    gather x8, local copies, waits for them, and re-layouts, accumulate(): jnp.take(fields, indices[3], axis=1)  157 us
    gather x8, local copies, waits for them, and re-layouts, accumulate(): jnp.take(fields, indices[2], axis=1)  154 us
    dot_general x44, matrix products, contract(): jnp.einsum(form, first_operand, second_operand, precision=lax.Precision.H...  141 us
    select_n x8, other arithmetic, accumulate(): jnp.take(fields, indices[2], axis=1)  99 us
    select_n x16, other arithmetic, accumulate(): jnp.take(fields, indices[3], axis=1)  73.6 us
    select_n x16, other arithmetic, accumulate(): jnp.take(fields, indices[1], axis=1)  73.6 us
    unnamed x95, local copies, waits for them, and re-layouts  71.8 us
  transfers between devices with their start and end apart: 21, of which 13 were waited for; matrix products, arithmetic and copies ran while one was open for 27% of the time, Pallas kernels for 0%

profile of v1, /device:TPU:18, one launch (start us, length us, event | category | flops | bytes accessed | tf_op | source)
XLA Modules:
  0.0 1722.5 jit_solution(17332745062665443782)
XLA Ops:
  18.4 44.6 %all-to-all-done = f32[4,1,131072]{2,1,0:T(1,128)S(1)} async-done(((f32[4,1,131072]{2,1,0:T(1,128)}), f32[4,1,131072]{2,1,0:T(1,128)S(1)}, u32[]{:S(2)}, u32[]{:S(2)}) %all-to-all-start) | async-done | bytes 2097184 | tf_op jit(solution)/shard_map/all_to_all | solution.py:42
  124.2 44.1 %all-to-all-done.1 = f32[4,1,131072]{2,1,0:T(1,128)} async-done(((f32[4,1,131072]{2,1,0:T(1,128)}), f32[4,1,131072]{2,1,0:T(1,128)}, u32[]{:S(2)}, u32[]{:S(2)}) %all-to-all-start.1) | async-done | bytes 2097184 | tf_op jit(solution)/shard_map/all_to_all | solution.py:69
  230.6 44.3 %all-to-all-done.2 = f32[4,1,131072]{2,1,0:T(1,128)} async-done(((f32[4,1,131072]{2,1,0:T(1,128)}), f32[4,1,131072]{2,1,0:T(1,128)}, u32[]{:S(2)}, u32[]{:S(2)}) %all-to-all-start.2) | async-done | bytes 2097184 | tf_op jit(solution)/shard_map/all_to_all | solution.py:100
  348.3 210.7 %while.44 = (s32[]{:T(128)}, f32[2,128,2048]{2,1,0:T(8,128)}, s32[2,4,512]{2,1,0:T(4,128)S(1)}, f32[2,512]{1,0:T(2,128)S(1)}, f32[2,128,2048]{2,0,1:T(2,128)S(1)}, /*index=5*/s32[]{:T(128)}, s32[]{:T(128)}, s32[]{}, s32[]{}, s32[]{}) while((s32[]{:T(128)}, f32[2,128,2048]{2,1,0:T(8,128)}, s32[2,4,512]{2,1,0:T(4,128)S(1)}, ...), condition=%wide.region_1.5_spmd.clone, body=%wide.region_0.4_spmd.clone.sunk | while | flops 3243000320 | bytes 234956048 | solution.py:136
  380.2 19.7 %gather_fusion.1 = f32[512,2,2048]{2,1,0:T(2,128)} fusion(f32[2,128,2048]{2,0,1:T(2,128)S(1)} %get-tuple-element.681, s32[1024]{0:T(1024)S(1)} %pad_clamp_fusion.25), kind=kCustom, calls=%fused_computation.clone.clone.1 | custom fusion | bytes 16779264 | tf_op jit(solution)/shard_map/while/body/eval_jaxpr/jit(_take)/gather | solution.py:127
  413.3 19.5 %gather_fusion.2 = f32[512,2,2048]{2,1,0:T(2,128)} fusion(f32[2,128,2048]{2,0,1:T(2,128)S(1)} %get-tuple-element.681, s32[1024]{0:T(1024)S(1)} %pad_clamp_fusion.26), kind=kCustom, calls=%fused_computation.2.clone.clone.1 | custom fusion | bytes 16779264 | tf_op jit(solution)/shard_map/while/body/eval_jaxpr/jit(_take)/gather | solution.py:129
  452.3 19.3 %gather_fusion = f32[512,2,2048]{2,1,0:T(2,128)} fusion(f32[2,128,2048]{2,0,1:T(2,128)S(1)} %get-tuple-element.681, s32[1024]{0:T(1024)S(1)} %pad_clamp_fusion.24), kind=kCustom, calls=%fused_computation.1.clone.clone.1 | custom fusion | bytes 16779264 | tf_op jit(solution)/shard_map/while/body/eval_jaxpr/jit(_take)/gather | solution.py:128
  484.0 19.5 %gather_fusion.1 = f32[512,2,2048]{2,1,0:T(2,128)} fusion(f32[2,128,2048]{2,0,1:T(2,128)S(1)} %get-tuple-element.681, s32[1024]{0:T(1024)S(1)} %pad_clamp_fusion.25), kind=kCustom, calls=%fused_computation.clone.clone.1 | custom fusion | bytes 16779264 | tf_op jit(solution)/shard_map/while/body/eval_jaxpr/jit(_take)/gather | solution.py:127
  516.9 19.8 %gather_fusion.2 = f32[512,2,2048]{2,1,0:T(2,128)} fusion(f32[2,128,2048]{2,0,1:T(2,128)S(1)} %get-tuple-element.681, s32[1024]{0:T(1024)S(1)} %pad_clamp_fusion.26), kind=kCustom, calls=%fused_computation.2.clone.clone.1 | custom fusion | bytes 16779264 | tf_op jit(solution)/shard_map/while/body/eval_jaxpr/jit(_take)/gather | solution.py:129
  563.5 225.8 %while.45 = (s32[]{:T(128)}, f32[2,128,2048]{2,1,0:T(8,128)}, s32[2,4,512]{2,1,0:T(4,128)S(1)}, f32[2,512]{1,0:T(2,128)S(1)}, f32[2,128,2048]{2,0,1:T(2,128)S(1)}, /*index=5*/s32[]{:T(128)}, s32[]{:T(128)}, s32[]{}, s32[]{}, s32[]{}) while((s32[]{:T(128)}, f32[2,128,2048]{2,1,0:T(8,128)}, s32[2,4,512]{2,1,0:T(4,128)S(1)}, ...), condition=%wide.region_3.7_spmd.clone, body=%wide.region_2.6_spmd.clone.sunk | while | flops 3243000320 | bytes 234956048 | solution.py:136
  598.3 30.0 %gather_fusion.4 = f32[512,2,2048]{2,1,0:T(2,128)} fusion(f32[2,128,2048]{2,0,1:T(2,128)S(1)} %get-tuple-element.711, s32[1024]{0:T(1024)S(1)} %pad_clamp_fusion.28), kind=kCustom, calls=%fused_computation.3.clone.clone.1 | custom fusion | bytes 16779264 | tf_op jit(solution)/shard_map/while/body/eval_jaxpr/jit(_take)/gather | solution.py:127
  641.7 19.8 %gather_fusion.5 = f32[512,2,2048]{2,1,0:T(2,128)} fusion(f32[2,128,2048]{2,0,1:T(2,128)S(1)} %get-tuple-element.711, s32[1024]{0:T(1024)S(1)} %pad_clamp_fusion.29), kind=kCustom, calls=%fused_computation.5.clone.clone.1 | custom fusion | bytes 16779264 | tf_op jit(solution)/shard_map/while/body/eval_jaxpr/jit(_take)/gather | solution.py:129
  712.4 19.7 %gather_fusion.4 = f32[512,2,2048]{2,1,0:T(2,128)} fusion(f32[2,128,2048]{2,0,1:T(2,128)S(1)} %get-tuple-element.711, s32[1024]{0:T(1024)S(1)} %pad_clamp_fusion.28), kind=kCustom, calls=%fused_computation.3.clone.clone.1 | custom fusion | bytes 16779264 | tf_op jit(solution)/shard_map/while/body/eval_jaxpr/jit(_take)/gather | solution.py:127
  745.5 19.5 %gather_fusion.5 = f32[512,2,2048]{2,1,0:T(2,128)} fusion(f32[2,128,2048]{2,0,1:T(2,128)S(1)} %get-tuple-element.711, s32[1024]{0:T(1024)S(1)} %pad_clamp_fusion.29), kind=kCustom, calls=%fused_computation.5.clone.clone.1 | custom fusion | bytes 16779264 | tf_op jit(solution)/shard_map/while/body/eval_jaxpr/jit(_take)/gather | solution.py:129
  796.3 30.6 %all_to_all.138 = f32[2,128,2048]{2,0,1:T(2,128)S(1)} all-to-all(f32[2,128,2048]{2,0,1:T(2,128)S(1)} %copy.154), channel_id=1, replica_groups=mesh['mode'=8,'tm'=4] {'mode'}, dimensions={1} | all-to-all | bytes 4194304 | tf_op jit(solution)/shard_map/all_to_all | solution.py:156
  864.2 52.5 %all_to_all.139 = f32[4,1,131072]{2,1,0:T(1,128)} all-to-all(f32[4,1,131072]{2,1,0:T(1,128)S(1)} %reshape.497), channel_id=1, replica_groups=mesh['mode'=8,'tm'=4] {'tm'}, dimensions={0} | all-to-all | bytes 4194304 | tf_op jit(solution)/shard_map/all_to_all | solution.py:69
  970.1 51.0 %all_to_all.140 = f32[4,1,131072]{2,1,0:T(1,128)} all-to-all(f32[4,1,131072]{2,1,0:T(1,128)S(1)} %reshape.499), channel_id=1, replica_groups=mesh['mode'=8,'tm'=4] {'tm'}, dimensions={0} | all-to-all | bytes 4194304 | tf_op jit(solution)/shard_map/all_to_all | solution.py:100
  1081.4 25.5 %collective-permute-done.9 = f32[2,16,2048]{2,1,0:T(8,128)S(1)} collective-permute-done((f32[2,16,2048]{2,1,0:T(8,128)S(1)}, f32[2,16,2048]{2,1,0:T(8,128)S(1)}, u32[]{:S(2)}, u32[]{:S(2)}) %collective-permute-start.9) | collective-permute-done | bytes 262176 | tf_op jit(solution)/shard_map/ppermute | solution.py:148
  1118.3 210.9 %while.46 = (s32[]{:T(128)}, f32[2,128,2048]{2,1,0:T(8,128)}, s32[2,4,512]{2,1,0:T(4,128)S(1)}, f32[2,512]{1,0:T(2,128)S(1)}, f32[2,128,2048]{2,0,1:T(2,128)S(1)}, /*index=5*/s32[]{:T(128)}, s32[]{:T(128)}, s32[]{}, s32[]{}, s32[]{}) while((s32[]{:T(128)}, f32[2,128,2048]{2,1,0:T(8,128)}, s32[2,4,512]{2,1,0:T(4,128)S(1)}, ...), condition=%wide.region_5.9_spmd.clone, body=%wide.region_4.8_spmd.clone.sunk | while | flops 3243000320 | bytes 234956048 | solution.py:136
  1150.5 19.5 %gather_fusion.7 = f32[512,2,2048]{2,1,0:T(2,128)} fusion(f32[2,128,2048]{2,0,1:T(2,128)S(1)} %get-tuple-element.741, s32[1024]{0:T(1024)S(1)} %pad_clamp_fusion.31), kind=kCustom, calls=%fused_computation.6.clone.clone.1 | custom fusion | bytes 16779264 | tf_op jit(solution)/shard_map/while/body/eval_jaxpr/jit(_take)/gather | solution.py:127
  1183.4 19.8 %gather_fusion.8 = f32[512,2,2048]{2,1,0:T(2,128)} fusion(f32[2,128,2048]{2,0,1:T(2,128)S(1)} %get-tuple-element.741, s32[1024]{0:T(1024)S(1)} %pad_clamp_fusion.32), kind=kCustom, calls=%fused_computation.8.clone.clone.1 | custom fusion | bytes 16779264 | tf_op jit(solution)/shard_map/while/body/eval_jaxpr/jit(_take)/gather | solution.py:129
  1222.4 19.3 %gather_fusion.6 = f32[512,2,2048]{2,1,0:T(2,128)} fusion(f32[2,128,2048]{2,0,1:T(2,128)S(1)} %get-tuple-element.741, s32[1024]{0:T(1024)S(1)} %pad_clamp_fusion.30), kind=kCustom, calls=%fused_computation.7.clone.clone.1 | custom fusion | bytes 16779264 | tf_op jit(solution)/shard_map/while/body/eval_jaxpr/jit(_take)/gather | solution.py:128
  1254.1 19.7 %gather_fusion.7 = f32[512,2,2048]{2,1,0:T(2,128)} fusion(f32[2,128,2048]{2,0,1:T(2,128)S(1)} %get-tuple-element.741, s32[1024]{0:T(1024)S(1)} %pad_clamp_fusion.31), kind=kCustom, calls=%fused_computation.6.clone.clone.1 | custom fusion | bytes 16779264 | tf_op jit(solution)/shard_map/while/body/eval_jaxpr/jit(_take)/gather | solution.py:127
  1287.2 19.5 %gather_fusion.8 = f32[512,2,2048]{2,1,0:T(2,128)} fusion(f32[2,128,2048]{2,0,1:T(2,128)S(1)} %get-tuple-element.741, s32[1024]{0:T(1024)S(1)} %pad_clamp_fusion.32), kind=kCustom, calls=%fused_computation.8.clone.clone.1 | custom fusion | bytes 16779264 | tf_op jit(solution)/shard_map/while/body/eval_jaxpr/jit(_take)/gather | solution.py:129
  1333.7 218.8 %while.47 = (s32[]{:T(128)}, f32[2,128,2048]{2,1,0:T(8,128)}, s32[2,4,512]{2,1,0:T(4,128)S(1)}, f32[2,512]{1,0:T(2,128)S(1)}, f32[2,128,2048]{2,0,1:T(2,128)S(1)}, /*index=5*/s32[]{:T(128)}, s32[]{:T(128)}, s32[]{}, s32[]{}, s32[]{}) while((s32[]{:T(128)}, f32[2,128,2048]{2,1,0:T(8,128)}, s32[2,4,512]{2,1,0:T(4,128)S(1)}, ...), condition=%wide.region_7.11_spmd.clone, body=%wide.region_6.10_spmd.clone.sunk | while | flops 3243000320 | bytes 234956048 | solution.py:136
  1368.4 19.8 %gather_fusion.10 = f32[512,2,2048]{2,1,0:T(2,128)} fusion(f32[2,128,2048]{2,0,1:T(2,128)S(1)} %get-tuple-element.771, s32[1024]{0:T(1024)S(1)} %pad_clamp_fusion.34), kind=kCustom, calls=%fused_computation.9.clone.clone.1 | custom fusion | bytes 16779264 | tf_op jit(solution)/shard_map/while/body/eval_jaxpr/jit(_take)/gather | solution.py:127
  1401.6 19.5 %gather_fusion.11 = f32[512,2,2048]{2,1,0:T(2,128)} fusion(f32[2,128,2048]{2,0,1:T(2,128)S(1)} %get-tuple-element.771, s32[1024]{0:T(1024)S(1)} %pad_clamp_fusion.35), kind=kCustom, calls=%fused_computation.11.clone.clone.1 | custom fusion | bytes 16779264 | tf_op jit(solution)/shard_map/while/body/eval_jaxpr/jit(_take)/gather | solution.py:129
  1440.6 19.3 %gather_fusion.9 = f32[512,2,2048]{2,1,0:T(2,128)} fusion(f32[2,128,2048]{2,0,1:T(2,128)S(1)} %get-tuple-element.771, s32[1024]{0:T(1024)S(1)} %pad_clamp_fusion.33), kind=kCustom, calls=%fused_computation.10.clone.clone.1 | custom fusion | bytes 16779264 | tf_op jit(solution)/shard_map/while/body/eval_jaxpr/jit(_take)/gather | solution.py:128
  1472.3 19.5 %gather_fusion.10 = f32[512,2,2048]{2,1,0:T(2,128)} fusion(f32[2,128,2048]{2,0,1:T(2,128)S(1)} %get-tuple-element.771, s32[1024]{0:T(1024)S(1)} %pad_clamp_fusion.34), kind=kCustom, calls=%fused_computation.9.clone.clone.1 | custom fusion | bytes 16779264 | tf_op jit(solution)/shard_map/while/body/eval_jaxpr/jit(_take)/gather | solution.py:127
  1505.2 19.8 %gather_fusion.11 = f32[512,2,2048]{2,1,0:T(2,128)} fusion(f32[2,128,2048]{2,0,1:T(2,128)S(1)} %get-tuple-element.771, s32[1024]{0:T(1024)S(1)} %pad_clamp_fusion.35), kind=kCustom, calls=%fused_computation.11.clone.clone.1 | custom fusion | bytes 16779264 | tf_op jit(solution)/shard_map/while/body/eval_jaxpr/jit(_take)/gather | solution.py:129
  1577.8 20.6 %all-to-all-done.6 = f32[2,128,2048]{2,0,1:T(2,128)S(1)} async-done(((f32[2,128,2048]{2,0,1:T(2,128)}), f32[2,128,2048]{2,0,1:T(2,128)S(1)}, u32[]{:S(2)}, u32[]{:S(2)}) %all-to-all-start.6) | async-done | bytes 2097184 | tf_op jit(solution)/shard_map/all_to_all | solution.py:156
  1657.9 39.8 %all-reduce = (f32[16]{0:T(128)S(1)}, f32[16]{0:T(128)S(1)}, f32[16]{0:T(128)S(1)}, f32[16]{0:T(128)S(1)}) all-reduce(f32[16]{0:T(128)S(1)} %reduce_sum.56, f32[16]{0:T(128)S(1)} %multiply_reduce_fusion, f32[16]{0:T(128)S(1)} %reduce_sum.52, f32[16]{0:T(128)S(1)} %multiply_reduce_fusion.2), channel_id=1, replica_groups=mesh['mode'=8,'tm'=4] {'tm'}, use_global_device_ids=true, to_apply=%region_15.19 | all-reduce | flops 64 | bytes 512 | tf_op jit(solution)/shard_map/psum | solution.py:177
  (437 shorter events, 959.1 us)
Async XLA Ops:
  12.9 50.1 %all-to-all-start = ((f32[4,1,131072]{2,1,0:T(1,128)}), f32[4,1,131072]{2,1,0:T(1,128)S(1)}, u32[]{:S(2)}, u32[]{:S(2)}) async-start(f32[4,1,131072]{2,1,0:T(1,128)} %reshape.491), calls=%async_computation | async-start | bytes 4194304 | tf_op jit(solution)/shard_map/all_to_all | solution.py:42
  18.4 86.5 %copy-start.30 = (f32[256,64]{0,1:T(8,128)}, f32[256,64]{0,1:T(8,128)S(1)}, u32[]{:S(2)}) copy-start(f32[256,64]{0,1:T(8,128)S(1)} %get-tuple-element.449) | copy-start | bytes 196612
  18.4 86.5 %copy-start.32 = (f32[256,64]{0,1:T(8,128)}, f32[256,64]{0,1:T(8,128)S(1)}, u32[]{:S(2)}) copy-start(f32[256,64]{0,1:T(8,128)S(1)} %get-tuple-element.450) | copy-start | bytes 196612
  110.5 13.2 copy-start.43
  116.1 52.2 %all-to-all-start.1 = ((f32[4,1,131072]{2,1,0:T(1,128)}), f32[4,1,131072]{2,1,0:T(1,128)}, u32[]{:S(2)}, u32[]{:S(2)}) async-start(f32[4,1,131072]{2,1,0:T(1,128)} %reshape.493), calls=%async_computation.1 | async-start | bytes 4194304 | tf_op jit(solution)/shard_map/all_to_all | solution.py:69
  123.8 74.3 %copy-start.36 = (f32[16]{0:T(128)}, f32[16]{0:T(128)S(1)}, u32[]{:S(2)}) copy-start(f32[16]{0:T(128)S(1)} %get-tuple-element.443) | copy-start | bytes 196
  123.8 74.3 %copy-start.38 = (f32[16]{0:T(128)}, f32[16]{0:T(128)S(1)}, u32[]{:S(2)}) copy-start(f32[16]{0:T(128)S(1)} %get-tuple-element.444) | copy-start | bytes 196
  123.8 74.3 %copy-start.40 = (f32[16]{0:T(128)}, f32[16]{0:T(128)S(1)}, u32[]{:S(2)}) copy-start(f32[16]{0:T(128)S(1)} %get-tuple-element.445) | copy-start | bytes 196
  124.2 74.0 %copy-start.28 = (f32[64,256]{1,0:T(8,128)}, f32[64,256]{1,0:T(8,128)S(1)}, u32[]{:S(2)}) copy-start(f32[64,256]{1,0:T(8,128)S(1)} %get-tuple-element.448) | copy-start | bytes 196612
  124.2 86.1 %copy-start.24 = (f32[64,256]{1,0:T(8,128)}, f32[64,256]{1,0:T(8,128)S(1)}, u32[]{:S(2)}) copy-start(f32[64,256]{1,0:T(8,128)S(1)} %get-tuple-element.446) | copy-start | bytes 196612
  124.2 86.1 %copy-start.26 = (f32[64,256]{1,0:T(8,128)}, f32[64,256]{1,0:T(8,128)S(1)}, u32[]{:S(2)}) copy-start(f32[64,256]{1,0:T(8,128)S(1)} %get-tuple-element.447) | copy-start | bytes 196612
  222.6 52.3 %all-to-all-start.2 = ((f32[4,1,131072]{2,1,0:T(1,128)}), f32[4,1,131072]{2,1,0:T(1,128)}, u32[]{:S(2)}, u32[]{:S(2)}) async-start(f32[4,1,131072]{2,1,0:T(1,128)} %reshape.495), calls=%async_computation.2 | async-start | bytes 4194304 | tf_op jit(solution)/shard_map/all_to_all | solution.py:100
  318.7 6.9 collective-permute-start
  318.7 14.0 collective-permute-start.1
  320.5 17.5 %collective-permute-start.2 = (f32[2,16,2048]{2,1,0:T(8,128)S(1)}, f32[2,16,2048]{2,1,0:T(8,128)S(1)}, u32[]{:S(2)}, u32[]{:S(2)}) collective-permute-start(f32[2,16,2048]{2,1,0:T(8,128)S(1)} %get-tuple-element.440), channel_id=1, source_target_pairs={{0,20},{4,24},{8,28},{12,0},{16,4},{20,8},{24,12},{28,16},{1,21},{... | collective-permute-start | bytes 786440 | tf_op jit(solution)/shard_map/ppermute | solution.py:148
  320.7 23.8 %collective-permute-start.3 = (f32[2,16,2048]{2,1,0:T(8,128)S(1)}, f32[2,16,2048]{2,1,0:T(8,128)S(1)}, u32[]{:S(2)}, u32[]{:S(2)}) collective-permute-start(f32[2,16,2048]{2,1,0:T(8,128)S(1)} %get-tuple-element.439), channel_id=1, source_target_pairs={{0,16},{4,20},{8,24},{12,28},{16,0},{20,4},{24,8},{28,12},{1,17},{... | collective-permute-start | bytes 786440 | tf_op jit(solution)/shard_map/ppermute | solution.py:148
  321.3 23.4 %collective-permute-start.4 = (f32[2,16,2048]{2,1,0:T(8,128)S(1)}, f32[2,16,2048]{2,1,0:T(8,128)S(1)}, u32[]{:S(2)}, u32[]{:S(2)}) collective-permute-start(f32[2,16,2048]{2,1,0:T(8,128)S(1)} %get-tuple-element.438), channel_id=1, source_target_pairs={{0,12},{4,16},{8,20},{12,24},{16,28},{20,0},{24,4},{28,8},{1,13},{... | collective-permute-start | bytes 786440 | tf_op jit(solution)/shard_map/ppermute | solution.py:148
  325.6 19.0 %collective-permute-start.5 = (f32[2,16,2048]{2,1,0:T(8,128)S(1)}, f32[2,16,2048]{2,1,0:T(8,128)S(1)}, u32[]{:S(2)}, u32[]{:S(2)}) collective-permute-start(f32[2,16,2048]{2,1,0:T(8,128)S(1)} %get-tuple-element.437), channel_id=1, source_target_pairs={{0,8},{4,12},{8,16},{12,20},{16,24},{20,28},{24,0},{28,4},{1,9},{5... | collective-permute-start | bytes 786440 | tf_op jit(solution)/shard_map/ppermute | solution.py:148
  332.8 12.0 collective-permute-start.6
  839.0 11.7 copy-start.33
  1064.7 14.6 collective-permute-start.7
  1064.7 15.6 collective-permute-start.8
  1069.9 490.8 %all-to-all-start.8 = ((f32[2,128,2048]{2,0,1:T(2,128)}), f32[2,128,2048]{2,0,1:T(2,128)}, u32[]{:S(2)}, u32[]{:S(2)}) async-start(f32[2,128,2048]{2,0,1:T(2,128)} %copy.173), calls=%async_computation.8 | async-start | bytes 4194304 | tf_op jit(solution)/shard_map/all_to_all | solution.py:157
  1075.4 31.5 %collective-permute-start.9 = (f32[2,16,2048]{2,1,0:T(8,128)S(1)}, f32[2,16,2048]{2,1,0:T(8,128)S(1)}, u32[]{:S(2)}, u32[]{:S(2)}) collective-permute-start(f32[2,16,2048]{2,1,0:T(8,128)S(1)} %get-tuple-element.431), channel_id=1, source_target_pairs={{0,20},{4,24},{8,28},{12,0},{16,4},{20,8},{24,12},{28,16},{1,21},{... | collective-permute-start | bytes 786440 | tf_op jit(solution)/shard_map/ppermute | solution.py:148
  1076.7 38.0 %collective-permute-start.10 = (f32[2,16,2048]{2,1,0:T(8,128)S(1)}, f32[2,16,2048]{2,1,0:T(8,128)S(1)}, u32[]{:S(2)}, u32[]{:S(2)}) collective-permute-start(f32[2,16,2048]{2,1,0:T(8,128)S(1)} %get-tuple-element.430), channel_id=1, source_target_pairs={{0,16},{4,20},{8,24},{12,28},{16,0},{20,4},{24,8},{28,12},{1,17},{... | collective-permute-start | bytes 786440 | tf_op jit(solution)/shard_map/ppermute | solution.py:148
  1077.2 37.4 %collective-permute-start.11 = (f32[2,16,2048]{2,1,0:T(8,128)S(1)}, f32[2,16,2048]{2,1,0:T(8,128)S(1)}, u32[]{:S(2)}, u32[]{:S(2)}) collective-permute-start(f32[2,16,2048]{2,1,0:T(8,128)S(1)} %get-tuple-element.429), channel_id=1, source_target_pairs={{0,12},{4,16},{8,20},{12,24},{16,28},{20,0},{24,4},{28,8},{1,13},{... | collective-permute-start | bytes 786440 | tf_op jit(solution)/shard_map/ppermute | solution.py:148
  1079.3 35.4 %collective-permute-start.12 = (f32[2,16,2048]{2,1,0:T(8,128)S(1)}, f32[2,16,2048]{2,1,0:T(8,128)S(1)}, u32[]{:S(2)}, u32[]{:S(2)}) collective-permute-start(f32[2,16,2048]{2,1,0:T(8,128)S(1)} %get-tuple-element.428), channel_id=1, source_target_pairs={{0,8},{4,12},{8,16},{12,20},{16,24},{20,28},{24,0},{28,4},{1,9},{5... | collective-permute-start | bytes 786440 | tf_op jit(solution)/shard_map/ppermute | solution.py:148
  1080.3 34.4 %collective-permute-start.13 = (f32[2,16,2048]{2,1,0:T(8,128)S(1)}, f32[2,16,2048]{2,1,0:T(8,128)S(1)}, u32[]{:S(2)}, u32[]{:S(2)}) collective-permute-start(f32[2,16,2048]{2,1,0:T(8,128)S(1)} %get-tuple-element.427), channel_id=1, source_target_pairs={{0,4},{4,8},{8,12},{12,16},{16,20},{20,24},{24,28},{28,0},{1,5},{5... | collective-permute-start | bytes 786440 | tf_op jit(solution)/shard_map/ppermute | solution.py:148
  1560.7 37.7 %all-to-all-start.6 = ((f32[2,128,2048]{2,0,1:T(2,128)}), f32[2,128,2048]{2,0,1:T(2,128)S(1)}, u32[]{:S(2)}, u32[]{:S(2)}) async-start(f32[2,128,2048]{2,0,1:T(2,128)} %copy.168), calls=%async_computation.6 | async-start | bytes 4194304 | tf_op jit(solution)/shard_map/all_to_all | solution.py:156
  1598.4 31.0 %all-to-all-start.9 = ((f32[2,128,2048]{2,0,1:T(2,128)}), f32[2,128,2048]{2,0,1:T(2,128)}, u32[]{:S(2)}, u32[]{:S(2)}) async-start(f32[2,128,2048]{2,0,1:T(2,128)} %copy.174), calls=%async_computation.9 | async-start | bytes 4194304 | tf_op jit(solution)/shard_map/all_to_all | solution.py:157
  1623.7 27.3 %copy-start.16 = (f32[2,128,2048]{2,0,1:T(2,128)S(1)}, f32[2,128,2048]{2,0,1:T(2,128)}, u32[]{:S(2)}) copy-start(f32[2,128,2048]{2,0,1:T(2,128)} %copy-done.15) | copy-start | bytes 6291460
  1629.4 68.9 %all-to-all-start.7 = ((f32[4,1,131072]{2,1,0:T(1,128)}), f32[4,1,131072]{2,1,0:T(1,128)}, u32[]{:S(2)}, u32[]{:S(2)}) async-start(f32[4,1,131072]{2,1,0:T(1,128)} %reshape.501), calls=%async_computation.7 | async-start | bytes 4194304 | tf_op jit(solution)/shard_map/all_to_all | solution.py:46
  (45 other events, 331.2 us)
